TPU v7x, 128 devices: a 2x2x16 block of a 8x8x16 slice. The times are simulated.
128 devices in a mesh: groups: 4 (over y, x), row: 32 (over z, core).
Axes of the slice: x: 2, y: 2, z: 16, core: 2. Of those that a mesh axis runs over, the one named last changes fastest.
The devices are a block of a 8x8x16 slice.
Arguments:
- design_matrix: bfloat16 [2048, 65536], P('groups', 'row'), parts along dimension 0, may hold values from -0.078125 to 0.078125
- targets: float32 [2048, 128], P(('groups', 'row')), parts along dimension 0, may hold values from -24 to 24
- linear: float32 [262144, 128], P(('groups', 'row')), parts along dimension 0, may hold values from -24 to 24
- diagonal: float32 [262144], P(('groups', 'row')), parts along dimension 0, may hold values from 0.1 to 2
- lower_code: int32 [262144, 128], P(('groups', 'row')), parts along dimension 0, may hold values from -192 to -17
- upper_code: int32 [262144, 128], P(('groups', 'row')), parts along dimension 0, may hold values from 16 to 191
Outputs:
- box_iterate: float32 [262144, 128], P(('groups', 'row')), parts along dimension 0
- scaled_dual: float32 [262144, 128], P(('groups', 'row')), parts along dimension 0
There are 4 independent parts, one for each index of `groups`. A program takes and returns all parts, laid end to end along the dimension named above; each array names one. Nothing has to cross between parts.
All inputs are finite; a program needn't handle non-finite values.
Results may differ from a plain program's by a relative error of at most 0.00033.
Values may be sent and summed in bfloat16 or wider, within the bound.
A program may use at most 128 MiB of HBM per device.

v0:
```python
import jax
import jax.numpy as jnp
from jax import lax
from jax.sharding import PartitionSpec as P

ITERS = 4


rho_plus_lip = 7.0


def in_blocks(value, dim, size):
    before, after = (value.shape[:dim], value.shape[dim + 1 :])
    return jnp.moveaxis(value.reshape(*before, size, -1, *after), dim, 0)


def sent_and_summed(value, axis, dim):
    size = lax.axis_size(axis)
    parts = lax.all_to_all(in_blocks(value, dim, size), axis, 0, 0, tiled=True)
    return jnp.sum(parts, axis=0)


def copy_for_each(value, axis):
    copies = jnp.broadcast_to(value, (lax.axis_size(axis), *value.shape))
    return lax.all_to_all(copies, axis, split_axis=0, concat_axis=0, tiled=True)


def laid_out(parts, dim):
    shape = list(parts.shape[1:])
    shape[dim] *= parts.shape[0]
    return jnp.moveaxis(parts, 0, dim).reshape(shape)


def gather_directly(value, axis, dim):
    parts = copy_for_each(value, axis)
    return laid_out(parts, dim)


def taken_together(value, axis):
    everything = copy_for_each(value, axis)
    return jnp.sum(everything, axis=0)


def solve_small(matrix, rhs):
    count = len(rhs)
    table = [list(line) for line in matrix]
    right = list(rhs)
    for p in range(count):
        for i in range(p + 1, count):
            factor = table[i][p] / table[p][p]
            for j in range(p, count):
                table[i][j] = table[i][j] - factor * table[p][j]
            right[i] = right[i] - factor * right[p]
    result = [None] * count
    for i in reversed(range(count)):
        total = right[i]
        for j in range(i + 1, count):
            total = total - table[i][j] * result[j]
        result[i] = total / table[i][i]
    return result


def mix_weights(gram):
    count = len(gram)
    trace = gram[0][0]
    for i in range(1, count):
        trace = trace + gram[i][i]
    shift = 0.01 * trace / count + 1e-06
    matrix = [[gram[i][j] + (shift if i == j else 0.0) for j in range(count)] for i in range(count)]
    solved = solve_small(matrix, [jnp.ones_like(trace)] * count)
    total = solved[0]
    for i in range(1, count):
        total = total + solved[i]
    return [item / total for item in solved]


def per_device(design_matrix, targets, linear, diagonal, lower_code, upper_code):
    lower = lower_code.astype(jnp.float32) / 64.0
    upper = upper_code.astype(jnp.float32) / 64.0
    step_size = (1.0 / (rho_plus_lip + diagonal))[:, None]
    state = jnp.zeros((2,) + linear.shape, jnp.float32)
    hist_mapped = []
    hist_change = []
    gram = []
    for iteration in range(ITERS):
        point = state[0] - state[1]
        point_b = point.astype(jnp.bfloat16)
        product = sent_and_summed(
            jnp.dot(design_matrix, point_b, preferred_element_type=jnp.float32), "row", 0
        )
        misfit = (product - targets).astype(jnp.bfloat16)
        gradient = lax.dot_general(
            design_matrix,
            gather_directly(misfit, "row", 0),
            (((0,), (0,)), ((), ())),
            preferred_element_type=jnp.float32,
        )
        gradient = gradient + diagonal[:, None] * point + linear
        moved = point - step_size * gradient
        boxed = jnp.clip(moved + state[1], lower, upper)
        scaled = state[1] + moved - boxed
        mapped = jnp.stack([boxed, scaled])
        change = mapped - state
        hist_mapped.append(mapped)
        hist_change.append(change)
        count = len(hist_change)
        stacked = jnp.stack(hist_change)
        partial_row = jnp.einsum("icns,cns->is", stacked, change, precision=lax.Precision.HIGHEST)
        newest = taken_together(partial_row, "row")
        for i in range(count - 1):
            gram[i].append(newest[i])
        gram.append([newest[i] for i in range(count)])
        alpha = mix_weights(gram)
        combined = alpha[0][None, None, :] * hist_mapped[0]
        for i in range(1, count):
            combined = combined + alpha[i][None, None, :] * hist_mapped[i]
        state = jnp.stack([jnp.clip(combined[0], lower, upper), combined[1]])
    return (state[0], state[1])


def solution(mesh):
    in_specs = (
        P("groups", "row"),
        P(("groups", "row"), None),
        P(("groups", "row"), None),
        P(("groups", "row")),
        P(("groups", "row"), None),
        P(("groups", "row"), None),
    )
    out_specs = (P(("groups", "row"), None), P(("groups", "row"), None))
    return jax.shard_map(
        per_device, mesh=mesh, in_specs=in_specs, out_specs=out_specs, check_vma=False
    )
```

profile of v0, /device:TPU:69, one launch (start us, length us, event | category | flops | bytes accessed | tf_op | source)
XLA Modules:
  0.0 457.7 jit_solution(8669930921941912975)
XLA Ops:
  0.7 1.6 copy-done
  3.2 40.4 %all_to_all.60 = f32[32,16,128]{2,1,0:T(8,128)S(1)} all-to-all(f32[32,16,128]{2,1,0:T(8,128)S(1)} %bitcast.415), channel_id=1, replica_groups=mesh['groups'=4,'row'=32] {'row'}, dimensions={0} | all-to-all | bytes 524288 | tf_op jit(solution)/shard_map/all_to_all | solution.py:19
  44.3 4.3 all-to-all-start.1
  48.7 1.6 copy.47
  50.2 2.5 copy.46
  52.8 2.5 copy.49
  55.3 9.3 %all-to-all-done.1 = bf16[32,16,128]{2,1,0:T(8,128)(2,1)S(1)} async-done(((bf16[32,16,128]{2,1,0:T(8,128)(2,1)}), bf16[32,16,128]{2,1,0:T(8,128)(2,1)S(1)}, u32[]{:S(2)}, u32[]{:S(2)}) %all-to-all-start.1) | async-done | bytes 131104 | tf_op jit(solution)/shard_map/all_to_all | solution.py:25
  64.6 2.2 fusion.45
  68.2 16.2 %all_to_all.61 = f32[32,1,128]{2,1,0:T(1,128)S(1)} all-to-all(f32[32,1,128]{2,1,0:T(1,128)S(1)} %broadcast_in_dim.17), channel_id=1, replica_groups=mesh['groups'=4,'row'=32] {'row'}, dimensions={0} | all-to-all | bytes 32768 | tf_op jit(solution)/shard_map/all_to_all | solution.py:25
  84.5 3.4 fusion.47
  88.1 1.1 copy-done.27
  89.2 1.0 copy-done.20
  91.9 26.1 %all_to_all.62 = f32[32,16,128]{2,1,0:T(8,128)S(1)} all-to-all(f32[32,16,128]{2,1,0:T(8,128)} %bitcast.416), channel_id=1, replica_groups=mesh['groups'=4,'row'=32] {'row'}, dimensions={0} | all-to-all | bytes 524288 | tf_op jit(solution)/shard_map/all_to_all | solution.py:19
  118.7 5.9 %all-to-all-start.4 = ((bf16[32,16,128]{2,1,0:T(8,128)(2,1)}), bf16[32,16,128]{2,1,0:T(8,128)(2,1)S(1)}, u32[]{:S(2)}, u32[]{:S(2)}) async-start(bf16[32,16,128]{2,1,0:T(8,128)(2,1)} %broadcast_in_dim.18), calls=%async_computation.4 | async-start | bytes 262144 | tf_op jit(solution)/shard_map/all_to_all | solution.py:25
  124.6 2.8 fusion.98
  127.4 12.7 %all-to-all-done.4 = bf16[32,16,128]{2,1,0:T(8,128)(2,1)S(1)} async-done(((bf16[32,16,128]{2,1,0:T(8,128)(2,1)}), bf16[32,16,128]{2,1,0:T(8,128)(2,1)S(1)}, u32[]{:S(2)}, u32[]{:S(2)}) %all-to-all-start.4) | async-done | bytes 131104 | tf_op jit(solution)/shard_map/all_to_all | solution.py:25
  140.1 2.6 fusion.24
  143.1 1.8 copy-done.21
  145.6 2.0 copy-done.12
  149.2 37.6 %fusion.4 = f32[128,1,2,1]{2,1,3,0:T(1,128)S(1)} fusion(f32[2,2,2048,128]{2,3,1,0:T(8,128)S(1)} %pad_maximum_fusion.2, f32[2,2048,128,1]{1,2,0,3:T(8,128)S(1)} %fusion.25), kind=kOutput, calls=%fused_computation.7 | convolution fusion | flops 12582912 | bytes 6292480 | tf_op jit(solution)/shard_map/icns,cns->is/dot_general | solution.py:108
  186.9 17.0 %all_to_all.63 = f32[32,2,128]{2,1,0:T(2,128)S(1)} all-to-all(f32[32,2,128]{2,1,0:T(2,128)S(1)} %broadcast_in_dim.19), channel_id=1, replica_groups=mesh['groups'=4,'row'=32] {'row'}, dimensions={0} | all-to-all | bytes 65536 | tf_op jit(solution)/shard_map/all_to_all | solution.py:25
  204.0 2.7 multiply_add_fusion.2
  207.0 1.1 copy-done.28
  210.8 26.2 %all_to_all.64 = f32[32,16,128]{2,1,0:T(8,128)S(1)} all-to-all(f32[32,16,128]{2,1,0:T(8,128)} %bitcast.417), channel_id=1, replica_groups=mesh['groups'=4,'row'=32] {'row'}, dimensions={0} | all-to-all | bytes 524288 | tf_op jit(solution)/shard_map/all_to_all | solution.py:19
  237.7 5.3 %all-to-all-start.7 = ((bf16[32,16,128]{2,1,0:T(8,128)(2,1)}), bf16[32,16,128]{2,1,0:T(8,128)(2,1)S(1)}, u32[]{:S(2)}, u32[]{:S(2)}) async-start(bf16[32,16,128]{2,1,0:T(8,128)(2,1)} %broadcast_in_dim.20), calls=%async_computation.7 | async-start | bytes 262144 | tf_op jit(solution)/shard_map/all_to_all | solution.py:25
  243.0 2.9 fusion.97
  245.9 13.0 %all-to-all-done.7 = bf16[32,16,128]{2,1,0:T(8,128)(2,1)S(1)} async-done(((bf16[32,16,128]{2,1,0:T(8,128)(2,1)}), bf16[32,16,128]{2,1,0:T(8,128)(2,1)S(1)}, u32[]{:S(2)}, u32[]{:S(2)}) %all-to-all-start.7) | async-done | bytes 131104 | tf_op jit(solution)/shard_map/all_to_all | solution.py:25
  258.9 2.6 fusion.19
  261.9 1.8 copy-done.23
  264.3 1.3 copy-done.13
  268.6 39.1 %fusion.2 = f32[128,1,3,1]{2,1,3,0:T(1,128)S(1)} fusion(f32[3,2,2048,128]{2,3,1,0:T(8,128)S(1)} %pad_maximum_fusion.1, f32[2,2048,128,1]{1,2,0,3:T(8,128)S(1)} %fusion.26), kind=kOutput, calls=%fused_computation.3 | convolution fusion | flops 18874368 | bytes 8390144 | tf_op jit(solution)/shard_map/icns,cns->is/dot_general | solution.py:108
  307.8 17.9 %all_to_all.65 = f32[32,3,128]{2,1,0:T(4,128)S(1)} all-to-all(f32[32,3,128]{2,1,0:T(4,128)S(1)} %broadcast_in_dim.21), channel_id=1, replica_groups=mesh['groups'=4,'row'=32] {'row'}, dimensions={0} | all-to-all | bytes 98304 | tf_op jit(solution)/shard_map/all_to_all | solution.py:25
  325.8 3.6 multiply_add_fusion.1
  329.8 1.2 copy-done.26
  333.6 26.4 %all_to_all.66 = f32[32,16,128]{2,1,0:T(8,128)S(1)} all-to-all(f32[32,16,128]{2,1,0:T(8,128)} %bitcast.418), channel_id=1, replica_groups=mesh['groups'=4,'row'=32] {'row'}, dimensions={0} | all-to-all | bytes 524288 | tf_op jit(solution)/shard_map/all_to_all | solution.py:19
  360.7 5.3 %all-to-all-start.10 = ((bf16[32,16,128]{2,1,0:T(8,128)(2,1)}), bf16[32,16,128]{2,1,0:T(8,128)(2,1)S(1)}, u32[]{:S(2)}, u32[]{:S(2)}) async-start(bf16[32,16,128]{2,1,0:T(8,128)(2,1)} %broadcast_in_dim.22), calls=%async_computation.10 | async-start | bytes 262144 | tf_op jit(solution)/shard_map/all_to_all | solution.py:25
  366.0 2.8 fusion.96
  368.8 13.1 %all-to-all-done.10 = bf16[32,16,128]{2,1,0:T(8,128)(2,1)S(1)} async-done(((bf16[32,16,128]{2,1,0:T(8,128)(2,1)}), bf16[32,16,128]{2,1,0:T(8,128)(2,1)S(1)}, u32[]{:S(2)}, u32[]{:S(2)}) %all-to-all-start.10) | async-done | bytes 131104 | tf_op jit(solution)/shard_map/all_to_all | solution.py:25
  381.9 2.5 fusion.14
  384.9 1.8 copy-done.19
  387.3 1.3 copy-done.14
  389.9 1.0 pad_maximum_fusion
  391.5 38.9 %fusion = f32[128,1,4,1]{2,1,3,0:T(1,128)S(1)} fusion(f32[4,2,2048,128]{2,3,1,0:T(8,128)S(1)} %pad_maximum_fusion, f32[2,2048,128,1]{1,2,0,3:T(8,128)S(1)} %fusion.27), kind=kOutput, calls=%fused_computation.1 | convolution fusion | flops 25165824 | bytes 10487808 | tf_op jit(solution)/shard_map/icns,cns->is/dot_general | solution.py:108
  430.5 17.7 %all_to_all.67 = f32[32,4,128]{2,1,0:T(4,128)S(1)} all-to-all(f32[32,4,128]{2,1,0:T(4,128)S(1)} %broadcast_in_dim.46), channel_id=1, replica_groups=mesh['groups'=4,'row'=32] {'row'}, dimensions={0} | all-to-all | bytes 131072 | tf_op jit(solution)/shard_map/all_to_all | solution.py:25
  448.4 4.0 multiply_add_fusion
  452.4 1.2 fusion.32
  453.7 1.3 copy.61
  455.0 2.5 copy.60
  (134 shorter events, 22.9 us)
Async XLA Ops:
  0.6 1.6 copy-start
  0.6 43.0 %copy-start.40 = (f32[16,128]{1,0:T(8,128)S(1)}, f32[16,128]{1,0:T(8,128)}, u32[]{:S(2)}) copy-start(f32[16,128]{1,0:T(8,128)} %param.7) | copy-start | bytes 24580
  44.3 20.2 %all-to-all-start.1 = ((bf16[32,16,128]{2,1,0:T(8,128)(2,1)}), bf16[32,16,128]{2,1,0:T(8,128)(2,1)S(1)}, u32[]{:S(2)}, u32[]{:S(2)}) async-start(bf16[32,16,128]{2,1,0:T(8,128)(2,1)} %broadcast_in_dim.16), calls=%async_computation.1 | async-start | bytes 262144 | tf_op jit(solution)/shard_map/all_to_all | solution.py:25
  50.2 5.1 %copy-start.39 = (f32[2048]{0:T(1024)S(1)}, f32[2048]{0:T(1024)}, u32[]{:S(2)}) copy-start(f32[2048]{0:T(1024)} %param.9) | copy-start | bytes 24580
  66.8 1.0 copy-start.9
  66.8 1.4 copy-start.10
  84.5 3.4 copy-start.1
  87.9 1.3 copy-start.27
  89.2 1.0 copy-start.20
  118.7 21.4 %all-to-all-start.4 = ((bf16[32,16,128]{2,1,0:T(8,128)(2,1)}), bf16[32,16,128]{2,1,0:T(8,128)(2,1)S(1)}, u32[]{:S(2)}, u32[]{:S(2)}) async-start(bf16[32,16,128]{2,1,0:T(8,128)(2,1)} %broadcast_in_dim.18), calls=%async_computation.4 | async-start | bytes 262144 | tf_op jit(solution)/shard_map/all_to_all | solution.py:25
  140.1 2.6 copy-start.2
  142.9 5.2 %copy-start.8 = (f32[2048,128]{0,1:T(8,128)}, f32[2048,128]{0,1:T(8,128)S(1)}, u32[]{:S(2)}) copy-start(f32[2048,128]{0,1:T(8,128)S(1)} %get-tuple-element.53) | copy-start | bytes 3145732
  143.0 5.2 %copy-start.24 = (f32[1,2048,128]{1,2,0:T(8,128)}, f32[1,2048,128]{1,2,0:T(8,128)S(1)}, u32[]{:S(2)}) copy-start(f32[1,2048,128]{1,2,0:T(8,128)S(1)} %get-tuple-element.52) | copy-start | bytes 3145732
  143.0 2.0 copy-start.21
  143.0 2.3 copy-start.38
  145.3 2.3 copy-start.12
  145.6 2.6 copy-start.15
  147.6 1.2 copy-start.34
  204.0 2.7 copy-start.3
  206.7 1.4 copy-start.28
  208.1 1.0 copy-start.22
  237.7 21.2 %all-to-all-start.7 = ((bf16[32,16,128]{2,1,0:T(8,128)(2,1)}), bf16[32,16,128]{2,1,0:T(8,128)(2,1)S(1)}, u32[]{:S(2)}, u32[]{:S(2)}) async-start(bf16[32,16,128]{2,1,0:T(8,128)(2,1)} %broadcast_in_dim.20), calls=%async_computation.7 | async-start | bytes 262144 | tf_op jit(solution)/shard_map/all_to_all | solution.py:25
  258.9 2.6 copy-start.4
  261.8 6.0 %copy-start.11 = (f32[2048,128]{0,1:T(8,128)}, f32[2048,128]{0,1:T(8,128)S(1)}, u32[]{:S(2)}) copy-start(f32[2048,128]{0,1:T(8,128)S(1)} %get-tuple-element.46) | copy-start | bytes 3145732
  261.8 2.0 copy-start.23
  261.8 2.3 copy-start.37
  261.9 5.8 %copy-start.31 = (f32[1,2048,128]{1,2,0:T(8,128)}, f32[1,2048,128]{1,2,0:T(8,128)S(1)}, u32[]{:S(2)}) copy-start(f32[1,2048,128]{1,2,0:T(8,128)S(1)} %subtract_bitcast_fusion.4) | copy-start | bytes 3145732
  264.1 1.6 copy-start.13
  264.1 2.2 copy-start.16
  266.3 1.5 copy-start.29
  266.3 2.0 copy-start.35
  325.8 3.7 copy-start.5
  329.5 1.4 copy-start.26
  330.9 1.0 copy-start.18
  360.7 21.2 %all-to-all-start.10 = ((bf16[32,16,128]{2,1,0:T(8,128)(2,1)}), bf16[32,16,128]{2,1,0:T(8,128)(2,1)S(1)}, u32[]{:S(2)}, u32[]{:S(2)}) async-start(bf16[32,16,128]{2,1,0:T(8,128)(2,1)} %broadcast_in_dim.22), calls=%async_computation.10 | async-start | bytes 262144 | tf_op jit(solution)/shard_map/all_to_all | solution.py:25
  381.9 2.6 copy-start.6
  384.7 6.2 %copy-start.25 = (f32[2048,128]{0,1:T(8,128)}, f32[2048,128]{0,1:T(8,128)S(1)}, u32[]{:S(2)}) copy-start(f32[2048,128]{0,1:T(8,128)S(1)} %get-tuple-element.33) | copy-start | bytes 3145732
  384.7 2.0 copy-start.19
  384.7 2.3 copy-start.36
  384.9 6.0 %copy-start.32 = (f32[1,2048,128]{1,2,0:T(8,128)}, f32[1,2048,128]{1,2,0:T(8,128)S(1)}, u32[]{:S(2)}) copy-start(f32[1,2048,128]{1,2,0:T(8,128)S(1)} %subtract_bitcast_fusion.2) | copy-start | bytes 3145732
  387.0 1.6 copy-start.14
  387.0 2.2 copy-start.17
  387.0 2.9 copy-start.30
  389.9 1.2 copy-start.33
  448.4 4.0 copy-start.7
where the time goes:
time: 465 us; the launch traced here: 458 us
  blocking collectives  188 us (40%)
  matrix products  129 us (28%)
  local copies, waits for them, and re-layouts  48.8 us (10%)
  waiting for transfers between devices  48.1 us (10%)
  other arithmetic  21.7 us (5%)
  starting transfers between devices  20.8 us (4%)
    all_to_all x4, blocking collectives, sent_and_summed(): parts = lax.all_to_all(in_blocks(value, dim, size), axis, 0, 0, tiled=True)  119 us
    dot_general x3, matrix products, per_device(): jnp.einsum('icns,cns->is', stacked, change, precision=lax.Precision.HIGHEST)  116 us
    all_to_all x4, blocking collectives, copy_for_each(): return lax.all_to_all(copies, axis, split_axis=0, concat_axis=0, tiled=True)  68.9 us
    all_to_all x4, waiting for transfers between devices, copy_for_each(): return lax.all_to_all(copies, axis, split_axis=0, concat_axis=0, tiled=True)  48.1 us
    unnamed x87, local copies, waits for them, and re-layouts  34.6 us
    all_to_all x4, starting transfers between devices, copy_for_each(): return lax.all_to_all(copies, axis, split_axis=0, concat_axis=0, tiled=True)  20.8 us
    add x3, other arithmetic, per_device(): combined = combined + alpha[i][None, None, :] * hist_mapped[i]  10.3 us
    dot_general x4, matrix products, per_device(): lax.dot_general(design_matrix, gather_directly(misfit, 'row', 0), (((0,),...  9.91 us
  transfers between devices with their start and end apart: 4, of which 4 were waited for; matrix products, arithmetic and copies ran while one was open for 3% of the time, Pallas kernels for 0%

commit v1 on v0

v1 whole, which is shorter than its diff:
```python
import functools

import jax
import jax.numpy as jnp
from jax import lax
from jax.experimental import pallas as pl
from jax.experimental.pallas import tpu as pltpu
from jax.sharding import PartitionSpec as P

ITERS = 4
WINDOW = 4
CHUNK = 256
rho_plus_lip = 7.0
F32, BF16 = jnp.float32, jnp.bfloat16
SENT_A, SENT_B = jnp.bfloat16, jnp.bfloat16


def solve_small(matrix, rhs):
    count = len(rhs)
    table = [list(line) for line in matrix]
    right = list(rhs)
    for p in range(count):
        for i in range(p + 1, count):
            factor = table[i][p] / table[p][p]
            for j in range(p, count):
                table[i][j] = table[i][j] - factor * table[p][j]
            right[i] = right[i] - factor * right[p]
    result = [None] * count
    for i in reversed(range(count)):
        total = right[i]
        for j in range(i + 1, count):
            total = total - table[i][j] * result[j]
        result[i] = total / table[i][i]
    return result


def mix_weights(gram):
    count = len(gram)
    trace = gram[0][0]
    for i in range(1, count):
        trace = trace + gram[i][i]
    shift = 0.01 * trace / count + 1e-06
    matrix = [[gram[i][j] + (shift if i == j else 0.0) for j in range(count)] for i in range(count)]
    solved = solve_small(matrix, [jnp.ones_like(trace)] * count)
    total = solved[0]
    for i in range(1, count):
        total = total + solved[i]
    return [item / total for item in solved]


def folded(value):
    return jnp.sum(value.reshape(-1, 8, value.shape[-1]), axis=0)


def kernel(
    devices,
    a_hbm, targets_hbm, linear_hbm, diagonal_hbm, lower_hbm, upper_hbm,
    z_hbm, u_hbm,
    a, a_t, linear, diagonal, code, low, high, dd, ss,
    mz, mu, cz, cu, sz, su, xb, pf, pb, known_a, ra, wb, known_b, window, m, targets, gp, ga, gw,
    load_sem, out_sem, send_sem, recv_sem,
):
    chips = devices // 2
    quarters = chips // WINDOW
    rows, n = a.shape
    block = rows // (2 * WINDOW)
    piece = block // quarters
    s = linear.shape[1]
    me = lax.axis_index("row")
    chip, core = me // 2, me % 2
    spot, quarter = chip % WINDOW, chip // WINDOW
    own = pl.multiple_of((2 * spot + core) * block, block)
    toward = 2 - 4 * core

    def at(offset, which):
        return 2 * ((chip + offset + chips) % chips) + which

    def owned_by(offset, which):
        return pl.multiple_of((2 * ((chip + offset + chips) % WINDOW) + which) * block, block)

    owners = [(at(0, 1 - core), owned_by(0, 1 - core), 0)]
    served = [at(0, 1 - core)]
    for offset, slot in ((1, 1), (-1, 3)):
        for which in (0, 1):
            owners.append((at(offset, which), owned_by(offset, which), slot + core))
            served.append(at(offset, which))
    for which in (0, 1):
        owners.append((at(toward, which), owned_by(toward, which), 5 + core))
    served += [at(-2, 0), at(2, 1)]
    sharers = [at(WINDOW * i, core) for i in range(1, quarters)]

    def send(source, target, device, index, arrival):
        copy = pltpu.make_async_remote_copy(
            src_ref=source,
            dst_ref=target,
            send_sem=send_sem.at[index],
            recv_sem=recv_sem.at[arrival],
            device_id={"row": device},
            device_id_type=pl.DeviceIdType.MESH,
        )
        copy.start()
        return copy

    def arrived(buffer, arrival):
        pltpu.make_async_remote_copy(
            src_ref=buffer,
            dst_ref=buffer,
            send_sem=send_sem.at[0],
            recv_sem=recv_sem.at[arrival],
            device_id={"row": at(0, 1 - core)},
            device_id_type=pl.DeviceIdType.MESH,
        ).wait_recv()

    def sent(copies):
        for copy in copies:
            copy.wait_send()

    def load(source, target, index):
        copy = pltpu.make_async_copy(source, target, load_sem.at[index])
        copy.start()
        return copy

    share = pl.ds(pl.multiple_of(quarter * piece, piece), piece)
    load_targets = load(targets_hbm, targets.at[share], 0)

    def load_a(i, carry):
        place, part = i // quarters, i % quarters
        source = pl.multiple_of((part * 2 * WINDOW + place) * piece, piece)
        target = pl.multiple_of(i * piece, piece)
        pltpu.make_async_copy(
            a_hbm.at[pl.ds(source, piece)], a.at[pl.ds(target, piece)], load_sem.at[1]
        ).start()
        return carry

    lax.fori_loop(0, 2 * WINDOW * quarters, load_a, 0)
    loads = [
        load(diagonal_hbm, diagonal, 2),
        load(lower_hbm, code.at[0], 3),
        load(upper_hbm, code.at[1], 4),
        load(linear_hbm, linear, 5),
    ]

    barrier = pltpu.get_barrier_semaphore()
    near = [at(0, 1 - core), at(1, 0), at(1, 1), at(-1, 0), at(-1, 1)]
    near += [at(toward, 0), at(toward, 1), at(-toward, core)]
    greeted = sharers + near
    for device in greeted:
        pl.semaphore_signal(
            barrier, inc=1, device_id={"row": device}, device_id_type=pl.DeviceIdType.MESH
        )

    load_targets.wait()
    pltpu.make_async_copy(a_hbm, a, load_sem.at[1]).wait()
    for copy in loads:
        copy.wait()

    def prepare(i, carry):
        part = pl.ds(pl.multiple_of(i * 128, 128), 128)
        a_t[part, :] = jnp.transpose(a[:, part])
        d = jnp.transpose(jnp.broadcast_to(diagonal[pl.ds(i, 1), :], (128, 128)))
        dd[part, :] = d
        ss[part, :] = 1.0 / (rho_plus_lip + d)
        low[part, :] = code[0, part, :].astype(F32) * (1.0 / 64.0)
        high[part, :] = code[1, part, :].astype(F32) * (1.0 / 64.0)
        return carry

    lax.fori_loop(0, n // 128, prepare, 0)
    pl.semaphore_wait(barrier, len(greeted))

    copies = [
        send(targets.at[share], targets.at[share], device, i, 0)
        for i, device in enumerate(sharers)
    ]
    arrived(targets.at[pl.ds(0, (quarters - 1) * piece)], 0)
    sent(copies)

    gram = []
    first = None
    for it in range(ITERS):
        mine = pl.ds(own, block)
        if it == 0:
            m[mine, :] = (0.0 - targets[...]).astype(BF16)
        else:
            def multiplied(i, carry):
                part = pl.ds(pl.multiple_of(i * 128, 128), 128)
                product = jnp.dot(a[part, :], xb[...], preferred_element_type=F32)
                pf[part, :] = product
                if it == 1:
                    rounded = product.astype(SENT_A)
                    known_a[part, :] = rounded.astype(F32)
                else:
                    known = known_a[part, :]
                    rounded = (product - known).astype(SENT_A)
                    known_a[part, :] = known + rounded.astype(F32)
                pb[part, :] = rounded
                return carry

            lax.fori_loop(0, rows // 128, multiplied, 0)
            copies = [
                send(pb.at[pl.ds(start, block)], ra.at[slot], device, i, 1)
                for i, (device, start, slot) in enumerate(owners)
            ]
            arrived(ra, 1)
            total = ra[0].astype(F32)
            for i in range(1, len(owners)):
                total = total + ra[i].astype(F32)
            if it > 1:
                total = total + window[...]
            window[...] = total
            total = total + pf[mine, :]
            if it > 1:
                total = total - known_b[0]
            rounded = total.astype(SENT_B)
            wb[quarter] = rounded
            known_b[0] = rounded.astype(F32) + (known_b[0] if it > 1 else 0.0)
            sent(copies)
            copies = [
                send(wb.at[quarter], wb.at[quarter], device, i, 2)
                for i, device in enumerate(sharers)
            ]
            arrived(wb.at[pl.ds(0, quarters - 1)], 2)
            sent(copies)
            total = wb[0].astype(F32)
            for i in range(1, quarters):
                total = total + wb[i].astype(F32)
            if it > 1:
                total = total + known_b[1]
            known_b[1] = total
            m[mine, :] = (total - targets[...]).astype(BF16)
        copies = [send(m.at[mine], m.at[mine], device, i, 3) for i, device in enumerate(served)]
        arrived(m.at[pl.ds(0, rows - block)], 3)
        sent(copies)

        def mapped(i, sums):
            part = pl.ds(pl.multiple_of(i * CHUNK, CHUNK), CHUNK)
            gradient = jnp.dot(a_t[part, :], m[...], preferred_element_type=F32)
            if it == 0:
                value = -ss[part, :] * (gradient + linear[part, :])
                z = jnp.minimum(jnp.maximum(value, low[part, :]), high[part, :])
                u = value - z
                mz[0, part, :] = z
                mu[0, part, :] = u
                xb[part, :] = (z - u).astype(BF16)
                return (sums[0] + folded(z * z + u * u),)
            z0, u0 = (mz[0, part, :], mu[0, part, :]) if it == 1 else (sz[part, :], su[part, :])
            point = z0 - u0
            gradient = gradient + dd[part, :] * point + linear[part, :]
            value = u0 + (point - ss[part, :] * gradient)
            z = jnp.minimum(jnp.maximum(value, low[part, :]), high[part, :])
            u = value - z
            mz[it, part, :] = z
            mu[it, part, :] = u
            dz, du = z - z0, u - u0
            if it < ITERS - 1:
                cz[it - 1, part, :] = dz
                cu[it - 1, part, :] = du
            out = []
            for j in range(it):
                pz, pu = (
                    (mz[0, part, :], mu[0, part, :])
                    if j == 0
                    else (cz[j - 1, part, :], cu[j - 1, part, :])
                )
                out.append(sums[j] + folded(pz * dz + pu * du))
            out.append(sums[it] + folded(dz * dz + du * du))
            return tuple(out)

        zero = jnp.zeros((8, s), F32)
        sums = lax.fori_loop(0, n // CHUNK, mapped, (zero,) * (it + 1))
        sums = [jnp.sum(item, axis=0, keepdims=True) for item in sums]
        if it == 0:
            first = sums[0]
            continue
        shared = ([first] if it == 1 else []) + sums
        for i in range(4):
            gp[pl.ds(i, 1), :] = shared[i] if i < len(shared) else jnp.zeros((1, s), F32)
        copies = [
            send(gp, ga.at[slot], device, i, 4) for i, (device, _, slot) in enumerate(owners)
        ]
        total = gp[...]
        arrived(ga, 4)
        for i in range(len(owners)):
            total = total + ga[i]
        gw[quarter] = total
        sent(copies)
        copies = [
            send(gw.at[quarter], gw.at[quarter], device, i, 5) for i, device in enumerate(sharers)
        ]
        arrived(gw.at[pl.ds(0, quarters - 1)], 5)
        sent(copies)
        total = gw[0]
        for i in range(1, quarters):
            total = total + gw[i]
        lines = [total[i : i + 1, :] for i in range(len(shared))]
        if it == 1:
            gram = [[lines[0]]]
            lines = lines[1:]
        for i in range(it):
            gram[i].append(lines[i])
        gram.append(lines)
        alpha = mix_weights(gram)

        def combined(i, carry):
            part = pl.ds(pl.multiple_of(i * CHUNK, CHUNK), CHUNK)
            z = alpha[0] * mz[0, part, :]
            u = alpha[0] * mu[0, part, :]
            for j in range(1, it + 1):
                z = z + alpha[j] * mz[j, part, :]
                u = u + alpha[j] * mu[j, part, :]
            z = jnp.minimum(jnp.maximum(z, low[part, :]), high[part, :])
            sz[part, :] = z
            su[part, :] = u
            if it < ITERS - 1:
                xb[part, :] = (z - u).astype(BF16)
            else:
                pltpu.make_async_copy(sz.at[part], z_hbm.at[part], out_sem.at[0]).start()
                pltpu.make_async_copy(su.at[part], u_hbm.at[part], out_sem.at[1]).start()
            return carry

        lax.fori_loop(0, n // CHUNK, combined, 0)
    pltpu.make_async_copy(sz, z_hbm, out_sem.at[0]).wait()
    pltpu.make_async_copy(su, u_hbm, out_sem.at[1]).wait()


def per_device(devices, design_matrix, targets, linear, diagonal, lower_code, upper_code):
    rows, n = design_matrix.shape
    s = linear.shape[1]
    quarters = devices // 2 // WINDOW
    block = rows // (2 * WINDOW)
    others = 2 * WINDOW - 1
    full = pltpu.VMEM((n, s), F32)
    hbm = pl.BlockSpec(memory_space=pl.ANY)
    return pl.pallas_call(
        functools.partial(kernel, devices),
        out_shape=(jax.ShapeDtypeStruct((n, s), F32),) * 2,
        in_specs=[hbm] * 6,
        out_specs=(hbm, hbm),
        scratch_shapes=[
            pltpu.VMEM((rows, n), BF16),
            pltpu.VMEM((n, rows), BF16),
            full,
            pltpu.VMEM((n // 128, 128), F32),
            pltpu.VMEM((2, n, s), jnp.int32),
            full,
            full,
            full,
            full,
            pltpu.VMEM((ITERS, n, s), F32),
            pltpu.VMEM((ITERS, n, s), F32),
            pltpu.VMEM((ITERS - 2, n, s), F32),
            pltpu.VMEM((ITERS - 2, n, s), F32),
            full,
            full,
            pltpu.VMEM((n, s), BF16),
            pltpu.VMEM((rows, s), F32),
            pltpu.VMEM((rows, s), SENT_A),
            pltpu.VMEM((rows, s), F32),
            pltpu.VMEM((others, block, s), SENT_A),
            pltpu.VMEM((quarters, block, s), SENT_B),
            pltpu.VMEM((2, block, s), F32),
            pltpu.VMEM((block, s), F32),
            pltpu.VMEM((rows, s), BF16),
            pltpu.VMEM((block, s), F32),
            pltpu.VMEM((4, s), F32),
            pltpu.VMEM((others, 4, s), F32),
            pltpu.VMEM((quarters, 4, s), F32),
            pltpu.SemaphoreType.DMA((6,)),
            pltpu.SemaphoreType.DMA((2,)),
            pltpu.SemaphoreType.DMA((others,)),
            pltpu.SemaphoreType.DMA((6,)),
        ],
        compiler_params=pltpu.CompilerParams(
            collective_id=0, has_side_effects=True, vmem_limit_bytes=56 * 1024 * 1024
        ),
        name="admm",
    )(
        design_matrix,
        targets,
        linear,
        diagonal.reshape(n // 128, 128),
        lower_code,
        upper_code,
    )


def solution(mesh):
    in_specs = (
        P("groups", "row"),
        P(("groups", "row"), None),
        P(("groups", "row"), None),
        P(("groups", "row")),
        P(("groups", "row"), None),
        P(("groups", "row"), None),
    )
    out_specs = (P(("groups", "row"), None), P(("groups", "row"), None))
    return jax.shard_map(
        functools.partial(per_device, mesh.shape["row"]),
        mesh=mesh,
        in_specs=in_specs,
        out_specs=out_specs,
        check_vma=False,
    )
```

time: 465 us -> 128 us (0.28); the launches traced: 458 us -> 127 us
  blocking collectives: 188 us -> 0 us
  matrix products: 129 us -> 0 us
  Pallas kernels: 0 us -> 124 us
  waiting for transfers between devices: 48.1 us -> 0 us
  local copies, waits for them, and re-layouts: 48.8 us -> 3.32 us
  other arithmetic: 21.7 us -> 0 us
  starting transfers between devices: 20.8 us -> 0 us
    all_to_all x8 -> x0, blocking collectives: 188 us -> none  [the longest x4 119 us: sent_and_summed(): parts = lax.all_to_all(in_blocks(value, dim, size), axis, 0, 0, tiled=True)]
    dot_general x11 -> x0, matrix products: 129 us -> none  [the longest x3 116 us: per_device(): jnp.einsum('icns,cns->is', stacked, change, precision=lax.Precision.HIGHEST)]
    pallas_call x0 -> x1, Pallas kernels: none -> 124 us  [per_device(): pl.pallas_call(functools.partial(kernel, devices), out_shape=(jax.ShapeDt...]
    all_to_all x4 -> x0, waiting for transfers between devices: 48.1 us -> none  [copy_for_each(): return lax.all_to_all(copies, axis, split_axis=0, concat_axis=0, tiled=True)]
    unnamed x87 -> x4, local copies, waits for them, and re-layouts: 34.6 us -> 3.32 us
    all_to_all x4 -> x0, starting transfers between devices: 20.8 us -> none  [copy_for_each(): return lax.all_to_all(copies, axis, split_axis=0, concat_axis=0, tiled=True)]
    add x3 -> x0, other arithmetic: 10.3 us -> none  [per_device(): combined = combined + alpha[i][None, None, :] * hist_mapped[i]]
    slice x3 -> x0, local copies, waits for them, and re-layouts: 8.49 us -> none  [per_device(): state = jnp.stack([jnp.clip(combined[0], lower, upper), combined[1]])]
  transfers between devices with their start and end apart: 4 -> 0, of which waited for: 4 -> 0; matrix products, arithmetic and copies ran while one was open for 3% -> 0% of each run, Pallas kernels for 0% -> 0%
where the time goes in v1:
time: 128 us; the launch traced here: 127 us
  Pallas kernels  124 us (97%)
  local copies, waits for them, and re-layouts  3.32 us (3%)
    pallas_call x1, Pallas kernels, per_device(): pl.pallas_call(functools.partial(kernel, devices), out_shape=(jax.ShapeDt...  124 us
    unnamed x4, local copies, waits for them, and re-layouts  3.32 us

profile of v1, /device:TPU:69, one launch (start us, length us, event | category | flops | bytes accessed | tf_op | source)
XLA Modules:
  0.0 127.5 jit_solution(13964133869765657853)
XLA Ops:
  0.6 123.5 %admm.1 = (f32[2048,128]{1,0:T(8,128)}, f32[2048,128]{1,0:T(8,128)}) custom-call(bf16[512,2048]{1,0:T(8,128)(2,1)} %a_hbm.1, f32[16,128]{1,0:T(8,128)} %targets_hbm.1, f32[2048,128]{1,0:T(8,128)} %linear_hbm.1, f32[16,128]{1,0:T(8,128)} %bitcast.1, s32[2048,128]{1,0:T(8,128)} %lower_hbm.1, s32[2048,128]{1,0:T(8,128)} %upper_hbm.1), custom_call_target="tpu_custom_call" | custom-call | tf_op jit(solution)/shard_map/admm/pallas_call | solution.py:333
  124.1 0.0 copy-start
  124.2 2.4 %copy.10 = f32[2048,128]{1,0:T(8,128)} copy(f32[2048,128]{1,0:T(8,128)} %get-tuple-element.4) | data formatting | bytes 2097152
  126.5 0.0 copy-done
  126.5 1.0 copy.11
Async XLA Ops:
  124.1 2.4 %copy-start = (f32[2048,128]{1,0:T(8,128)S(1)}, f32[2048,128]{1,0:T(8,128)}, u32[]{:S(2)}) copy-start(f32[2048,128]{1,0:T(8,128)} %get-tuple-element.5) | copy-start | bytes 3145732

commit v2 on v1

--- a/solution.py
+++ b/solution.py
@@ -19,10 +19,12 @@
     count = len(rhs)
     table = [list(line) for line in matrix]
     right = list(rhs)
+    inverse = []
     for p in range(count):
+        inverse.append(1.0 / table[p][p])
         for i in range(p + 1, count):
-            factor = table[i][p] / table[p][p]
-            for j in range(p, count):
+            factor = table[i][p] * inverse[p]
+            for j in range(p + 1, count):
                 table[i][j] = table[i][j] - factor * table[p][j]
             right[i] = right[i] - factor * right[p]
     result = [None] * count
@@ -30,7 +32,7 @@
         total = right[i]
         for j in range(i + 1, count):
             total = total - table[i][j] * result[j]
-        result[i] = total / table[i][i]
+        result[i] = total * inverse[i]
     return result
 
 
@@ -45,7 +47,8 @@
     total = solved[0]
     for i in range(1, count):
         total = total + solved[i]
-    return [item / total for item in solved]
+    inverse = 1.0 / total
+    return [item * inverse for item in solved]
 
 
 def folded(value):
@@ -57,7 +60,7 @@
     a_hbm, targets_hbm, linear_hbm, diagonal_hbm, lower_hbm, upper_hbm,
     z_hbm, u_hbm,
     a, a_t, linear, diagonal, code, low, high, dd, ss,
-    mz, mu, cz, cu, sz, su, xb, pf, pb, known_a, ra, wb, known_b, window, m, targets, gp, ga, gw,
+    mz, mu, cz, cu, sz, su, base, xb, pf, pb, known_a, ra, wb, known_b, window, m, targets, ga_1, ga_2, ga_3,
     load_sem, out_sem, send_sem, recv_sem,
 ):
     chips = devices // 2
@@ -78,15 +81,31 @@
     def owned_by(offset, which):
         return pl.multiple_of((2 * ((chip + offset + chips) % WINDOW) + which) * block, block)
 
-    owners = [(at(0, 1 - core), owned_by(0, 1 - core), 0)]
-    served = [at(0, 1 - core)]
-    for offset, slot in ((1, 1), (-1, 3)):
+    served = [at(-2, 0), at(2, 1)]
+    for offset in (1, -1):
         for which in (0, 1):
-            owners.append((at(offset, which), owned_by(offset, which), slot + core))
             served.append(at(offset, which))
-    for which in (0, 1):
-        owners.append((at(toward, which), owned_by(toward, which), 5 + core))
-    served += [at(-2, 0), at(2, 1)]
+    served.append(at(0, 1 - core))
+    def everyone(source, target, arrival):
+        def chips_away(i, carry):
+            away = (chips // 2 - (i + 1) // 2) * (1 - 2 * ((i + 1) % 2))
+            for which in (0, 1):
+                send(source, target, at(away, which), arrival, arrival)
+            return carry
+
+        lax.fori_loop(0, chips - 1, chips_away, 0)
+        send(source, target, at(0, 1 - core), arrival, arrival)
+
+    def left(buffer, index):
+        pltpu.make_async_remote_copy(
+            src_ref=buffer,
+            dst_ref=buffer,
+            send_sem=send_sem.at[index],
+            recv_sem=recv_sem.at[0],
+            device_id={"row": at(0, 1 - core)},
+            device_id_type=pl.DeviceIdType.MESH,
+        ).wait_send()
+
     sharers = [at(WINDOW * i, core) for i in range(1, quarters)]
 
     def send(source, target, device, index, arrival):
@@ -111,14 +130,24 @@
             device_id_type=pl.DeviceIdType.MESH,
         ).wait_recv()
 
-    def sent(copies):
-        for copy in copies:
-            copy.wait_send()
-
     def load(source, target, index):
         copy = pltpu.make_async_copy(source, target, load_sem.at[index])
         copy.start()
         return copy
+
+    barrier = pltpu.get_barrier_semaphore()
+
+    def greet(i, carry):
+        away = (devices // 2 - (i + 1) // 2) * (1 - 2 * ((i + 1) % 2))
+        pl.semaphore_signal(
+            barrier,
+            inc=1,
+            device_id={"row": (me + away + devices) % devices},
+            device_id_type=pl.DeviceIdType.MESH,
+        )
+        return carry
+
+    lax.fori_loop(0, devices - 1, greet, 0)
 
     share = pl.ds(pl.multiple_of(quarter * piece, piece), piece)
     load_targets = load(targets_hbm, targets.at[share], 0)
@@ -140,16 +169,14 @@
         load(linear_hbm, linear, 5),
     ]
 
-    barrier = pltpu.get_barrier_semaphore()
-    near = [at(0, 1 - core), at(1, 0), at(1, 1), at(-1, 0), at(-1, 1)]
-    near += [at(toward, 0), at(toward, 1), at(-toward, core)]
-    greeted = sharers + near
-    for device in greeted:
-        pl.semaphore_signal(
-            barrier, inc=1, device_id={"row": device}, device_id_type=pl.DeviceIdType.MESH
-        )
-
+    shown = pl.ds(pl.multiple_of(own + quarter * piece, piece), piece)
     load_targets.wait()
+    m[shown, :] = (0.0 - targets[share, :]).astype(BF16)
+    pl.semaphore_wait(barrier, devices - 1)
+    everyone(m.at[shown], m.at[shown], 3)
+    for device in sharers:
+        send(targets.at[share], targets.at[share], device, 0, 0)
+
     pltpu.make_async_copy(a_hbm, a, load_sem.at[1]).wait()
     for copy in loads:
         copy.wait()
@@ -165,24 +192,19 @@
         return carry
 
     lax.fori_loop(0, n // 128, prepare, 0)
-    pl.semaphore_wait(barrier, len(greeted))
-
-    copies = [
-        send(targets.at[share], targets.at[share], device, i, 0)
-        for i, device in enumerate(sharers)
-    ]
-    arrived(targets.at[pl.ds(0, (quarters - 1) * piece)], 0)
-    sent(copies)
-
+
+    arrived(m.at[pl.ds(0, rows - piece)], 3)
+    left(m.at[pl.ds(0, rows - piece)], 3)
+
+    gas = [ga_1, ga_2, ga_3]
     gram = []
     first = None
     for it in range(ITERS):
         mine = pl.ds(own, block)
-        if it == 0:
-            m[mine, :] = (0.0 - targets[...]).astype(BF16)
-        else:
+        if it > 0:
             def multiplied(i, carry):
-                part = pl.ds(pl.multiple_of(i * 128, 128), 128)
+                offset = jnp.where(i == 0, toward, jnp.where(i == 3, 0, 3 - 2 * i))
+                part = pl.ds(pl.multiple_of(owned_by(offset, 0), 2 * block), 2 * block)
                 product = jnp.dot(a[part, :], xb[...], preferred_element_type=F32)
                 pf[part, :] = product
                 if it == 1:
@@ -193,16 +215,33 @@
                     rounded = (product - known).astype(SENT_A)
                     known_a[part, :] = known + rounded.astype(F32)
                 pb[part, :] = rounded
+
+                @pl.when(i < WINDOW - 1)
+                def _():
+                    for which in (0, 1):
+                        send(
+                            pb.at[pl.ds(owned_by(offset, which), block)],
+                            ra.at[2 * ((i + 2) % 3) + 1 + core],
+                            at(offset, which),
+                            1,
+                            1,
+                        )
+
                 return carry
 
-            lax.fori_loop(0, rows // 128, multiplied, 0)
-            copies = [
-                send(pb.at[pl.ds(start, block)], ra.at[slot], device, i, 1)
-                for i, (device, start, slot) in enumerate(owners)
-            ]
+            def based(i, carry):
+                part = pl.ds(pl.multiple_of(i * CHUNK, CHUNK), CHUNK)
+                z0, u0 = (mz[0, part, :], mu[0, part, :]) if it == 1 else (sz[part, :], su[part, :])
+                point = z0 - u0
+                base[part, :] = z0 - ss[part, :] * (dd[part, :] * point + linear[part, :])
+                return carry
+
+            lax.fori_loop(0, WINDOW, multiplied, 0)
+            send(pb.at[pl.ds(owned_by(0, 1 - core), block)], ra.at[0], at(0, 1 - core), 1, 1)
+            lax.fori_loop(0, n // CHUNK, based, 0)
             arrived(ra, 1)
             total = ra[0].astype(F32)
-            for i in range(1, len(owners)):
+            for i in range(1, len(served)):
                 total = total + ra[i].astype(F32)
             if it > 1:
                 total = total + window[...]
@@ -213,23 +252,25 @@
             rounded = total.astype(SENT_B)
             wb[quarter] = rounded
             known_b[0] = rounded.astype(F32) + (known_b[0] if it > 1 else 0.0)
-            sent(copies)
-            copies = [
-                send(wb.at[quarter], wb.at[quarter], device, i, 2)
-                for i, device in enumerate(sharers)
-            ]
+            for device in sharers:
+                send(wb.at[quarter], wb.at[quarter], device, 2, 2)
+            left(ra, 1)
             arrived(wb.at[pl.ds(0, quarters - 1)], 2)
-            sent(copies)
             total = wb[0].astype(F32)
             for i in range(1, quarters):
                 total = total + wb[i].astype(F32)
             if it > 1:
                 total = total + known_b[1]
             known_b[1] = total
+            if it == 1:
+                arrived(targets.at[pl.ds(0, (quarters - 1) * piece)], 0)
+                left(targets.at[pl.ds(0, (quarters - 1) * piece)], 0)
             m[mine, :] = (total - targets[...]).astype(BF16)
-        copies = [send(m.at[mine], m.at[mine], device, i, 3) for i, device in enumerate(served)]
-        arrived(m.at[pl.ds(0, rows - block)], 3)
-        sent(copies)
+            for device in served:
+                send(m.at[mine], m.at[mine], device, 3, 3)
+            left(wb.at[pl.ds(0, quarters - 1)], 2)
+            arrived(m.at[pl.ds(0, rows - block)], 3)
+            left(m.at[pl.ds(0, rows - block)], 3)
 
         def mapped(i, sums):
             part = pl.ds(pl.multiple_of(i * CHUNK, CHUNK), CHUNK)
@@ -243,9 +284,7 @@
                 xb[part, :] = (z - u).astype(BF16)
                 return (sums[0] + folded(z * z + u * u),)
             z0, u0 = (mz[0, part, :], mu[0, part, :]) if it == 1 else (sz[part, :], su[part, :])
-            point = z0 - u0
-            gradient = gradient + dd[part, :] * point + linear[part, :]
-            value = u0 + (point - ss[part, :] * gradient)
+            value = base[part, :] - ss[part, :] * gradient
             z = jnp.minimum(jnp.maximum(value, low[part, :]), high[part, :])
             u = value - z
             mz[it, part, :] = z
@@ -272,25 +311,13 @@
             first = sums[0]
             continue
         shared = ([first] if it == 1 else []) + sums
-        for i in range(4):
-            gp[pl.ds(i, 1), :] = shared[i] if i < len(shared) else jnp.zeros((1, s), F32)
-        copies = [
-            send(gp, ga.at[slot], device, i, 4) for i, (device, _, slot) in enumerate(owners)
-        ]
-        total = gp[...]
-        arrived(ga, 4)
-        for i in range(len(owners)):
-            total = total + ga[i]
-        gw[quarter] = total
-        sent(copies)
-        copies = [
-            send(gw.at[quarter], gw.at[quarter], device, i, 5) for i, device in enumerate(sharers)
-        ]
-        arrived(gw.at[pl.ds(0, quarters - 1)], 5)
-        sent(copies)
-        total = gw[0]
-        for i in range(1, quarters):
-            total = total + gw[i]
+        ga = gas[it - 1]
+        for i in range(len(shared)):
+            ga[me, pl.ds(i, 1), :] = shared[i]
+        everyone(ga.at[me], ga.at[me], 4)
+        arrived(ga.at[pl.ds(0, devices - 1)], 4)
+        total = jnp.sum(ga[...], axis=0)
+        left(ga.at[pl.ds(0, devices - 1)], 4)
         lines = [total[i : i + 1, :] for i in range(len(shared))]
         if it == 1:
             gram = [[lines[0]]]
@@ -308,18 +335,16 @@
                 z = z + alpha[j] * mz[j, part, :]
                 u = u + alpha[j] * mu[j, part, :]
             z = jnp.minimum(jnp.maximum(z, low[part, :]), high[part, :])
-            sz[part, :] = z
-            su[part, :] = u
             if it < ITERS - 1:
+                sz[part, :] = z
+                su[part, :] = u
                 xb[part, :] = (z - u).astype(BF16)
             else:
-                pltpu.make_async_copy(sz.at[part], z_hbm.at[part], out_sem.at[0]).start()
-                pltpu.make_async_copy(su.at[part], u_hbm.at[part], out_sem.at[1]).start()
+                z_hbm[part, :] = z
+                u_hbm[part, :] = u
             return carry
 
         lax.fori_loop(0, n // CHUNK, combined, 0)
-    pltpu.make_async_copy(sz, z_hbm, out_sem.at[0]).wait()
-    pltpu.make_async_copy(su, u_hbm, out_sem.at[1]).wait()
 
 
 def per_device(devices, design_matrix, targets, linear, diagonal, lower_code, upper_code):
@@ -332,9 +357,9 @@
     hbm = pl.BlockSpec(memory_space=pl.ANY)
     return pl.pallas_call(
         functools.partial(kernel, devices),
-        out_shape=(jax.ShapeDtypeStruct((n, s), F32),) * 2,
+        out_shape=(pltpu.VMEM((n, s), F32),) * 2,
         in_specs=[hbm] * 6,
-        out_specs=(hbm, hbm),
+        out_specs=(pl.BlockSpec(memory_space=pltpu.VMEM),) * 2,
         scratch_shapes=[
             pltpu.VMEM((rows, n), BF16),
             pltpu.VMEM((n, rows), BF16),
@@ -349,6 +374,7 @@
             pltpu.VMEM((ITERS, n, s), F32),
             pltpu.VMEM((ITERS - 2, n, s), F32),
             pltpu.VMEM((ITERS - 2, n, s), F32),
+            full,
             full,
             full,
             pltpu.VMEM((n, s), BF16),
@@ -361,13 +387,13 @@
             pltpu.VMEM((block, s), F32),
             pltpu.VMEM((rows, s), BF16),
             pltpu.VMEM((block, s), F32),
-            pltpu.VMEM((4, s), F32),
-            pltpu.VMEM((others, 4, s), F32),
-            pltpu.VMEM((quarters, 4, s), F32),
+            pltpu.VMEM((devices, 3, s), F32),
+            pltpu.VMEM((devices, 3, s), F32),
+            pltpu.VMEM((devices, 4, s), F32),
             pltpu.SemaphoreType.DMA((6,)),
             pltpu.SemaphoreType.DMA((2,)),
-            pltpu.SemaphoreType.DMA((others,)),
-            pltpu.SemaphoreType.DMA((6,)),
+            pltpu.SemaphoreType.DMA((5,)),
+            pltpu.SemaphoreType.DMA((5,)),
         ],
         compiler_params=pltpu.CompilerParams(
             collective_id=0, has_side_effects=True, vmem_limit_bytes=56 * 1024 * 1024

time: 128 us -> 108 us (0.84)
  Pallas kernels: 124 us -> 105 us
  local copies, waits for them, and re-layouts: 3.32 us -> 1.94 us
    pallas_call x1, Pallas kernels: 124 us -> 105 us  [per_device(): pl.pallas_call(functools.partial(kernel, devices), out_shape=(pltpu.VMEM(...]
    unnamed x4 -> x2, local copies, waits for them, and re-layouts: 3.32 us -> 1.94 us
where the time goes in v2:
time: 108 us
  Pallas kernels  105 us (97%)
  local copies, waits for them, and re-layouts  1.94 us (2%)
    pallas_call x1, Pallas kernels, per_device(): pl.pallas_call(functools.partial(kernel, devices), out_shape=(pltpu.VMEM(...  105 us

profile of v2, /device:TPU:69, one launch (start us, length us, event | category | flops | bytes accessed | tf_op | source)
XLA Modules:
  0.0 108.0 jit_solution(11736578669005856229)
XLA Ops:
  0.6 105.5 %admm.1 = (f32[2048,128]{1,0:T(8,128)S(1)}, f32[2048,128]{1,0:T(8,128)S(1)}) custom-call(bf16[512,2048]{1,0:T(8,128)(2,1)} %a_hbm.1, f32[16,128]{1,0:T(8,128)} %targets_hbm.1, f32[2048,128]{1,0:T(8,128)} %linear_hbm.1, f32[16,128]{1,0:T(8,128)} %bitcast.1, s32[2048,128]{1,0:T(8,128)} %lower_hbm.1, s32[2048,128]{1,0:T(8,128)} %upper_hbm.1), custom_call_target="tpu_custom_call" | custom-call | tf_op jit(solution)/shard_map/admm/pallas_call | solution.py:358
  106.1 1.0 copy.10
  107.1 1.0 copy.11

commit v3 on v2

--- a/solution.py
+++ b/solution.py
@@ -9,7 +9,7 @@
 
 ITERS = 4
 WINDOW = 4
-CHUNK = 256
+CHUNK = 1024
 rho_plus_lip = 7.0
 F32, BF16 = jnp.float32, jnp.bfloat16
 SENT_A, SENT_B = jnp.bfloat16, jnp.bfloat16

time: 108 us -> 104 us (0.963)
  Pallas kernels: 105 us -> 102 us
    pallas_call x1, Pallas kernels: 105 us -> 102 us  [per_device(): pl.pallas_call(functools.partial(kernel, devices), out_shape=(pltpu.VMEM(...]
where the time goes in v3:
time: 104 us
  Pallas kernels  102 us (98%)
  local copies, waits for them, and re-layouts  1.94 us (2%)
    pallas_call x1, Pallas kernels, per_device(): pl.pallas_call(functools.partial(kernel, devices), out_shape=(pltpu.VMEM(...  102 us

profile of v3, /device:TPU:69, one launch (start us, length us, event | category | flops | bytes accessed | tf_op | source)
XLA Modules:
  0.0 104.1 jit_solution(8383216895353937758)
XLA Ops:
  0.6 101.5 %admm.1 = (f32[2048,128]{1,0:T(8,128)S(1)}, f32[2048,128]{1,0:T(8,128)S(1)}) custom-call(bf16[512,2048]{1,0:T(8,128)(2,1)} %a_hbm.1, f32[16,128]{1,0:T(8,128)} %targets_hbm.1, f32[2048,128]{1,0:T(8,128)} %linear_hbm.1, f32[16,128]{1,0:T(8,128)} %bitcast.1, s32[2048,128]{1,0:T(8,128)} %lower_hbm.1, s32[2048,128]{1,0:T(8,128)} %upper_hbm.1), custom_call_target="tpu_custom_call" | custom-call | tf_op jit(solution)/shard_map/admm/pallas_call | solution.py:358
  102.1 1.0 copy.10
  103.1 1.0 copy.11

commit v4 on v3

--- a/solution.py
+++ b/solution.py
@@ -106,7 +106,7 @@
             device_id_type=pl.DeviceIdType.MESH,
         ).wait_send()
 
-    sharers = [at(WINDOW * i, core) for i in range(1, quarters)]
+    sharers = [at(WINDOW * i, core) for i in (2, 1, 3)]
 
     def send(source, target, device, index, arrival):
         copy = pltpu.make_async_remote_copy(
@@ -238,7 +238,6 @@
 
             lax.fori_loop(0, WINDOW, multiplied, 0)
             send(pb.at[pl.ds(owned_by(0, 1 - core), block)], ra.at[0], at(0, 1 - core), 1, 1)
-            lax.fori_loop(0, n // CHUNK, based, 0)
             arrived(ra, 1)
             total = ra[0].astype(F32)
             for i in range(1, len(served)):
@@ -252,7 +251,9 @@
             rounded = total.astype(SENT_B)
             wb[quarter] = rounded
             known_b[0] = rounded.astype(F32) + (known_b[0] if it > 1 else 0.0)
-            for device in sharers:
+            send(wb.at[quarter], wb.at[quarter], sharers[0], 2, 2)
+            lax.fori_loop(0, n // CHUNK, based, 0)
+            for device in sharers[1:]:
                 send(wb.at[quarter], wb.at[quarter], device, 2, 2)
             left(ra, 1)
             arrived(wb.at[pl.ds(0, quarters - 1)], 2)

time: 104 us -> 103 us (level)
  Pallas kernels: 102 us -> 100 us
    pallas_call x1, Pallas kernels: 102 us -> 100 us  [per_device(): pl.pallas_call(functools.partial(kernel, devices), out_shape=(pltpu.VMEM(...]
where the time goes in v4:
time: 103 us
  Pallas kernels  100 us (97%)
  local copies, waits for them, and re-layouts  1.94 us (2%)
    pallas_call x1, Pallas kernels, per_device(): pl.pallas_call(functools.partial(kernel, devices), out_shape=(pltpu.VMEM(...  100 us

profile of v4, /device:TPU:69, one launch (start us, length us, event | category | flops | bytes accessed | tf_op | source)
XLA Modules:
  0.0 102.6 jit_solution(9872108310232708899)
XLA Ops:
  0.6 100.1 %admm.1 = (f32[2048,128]{1,0:T(8,128)S(1)}, f32[2048,128]{1,0:T(8,128)S(1)}) custom-call(bf16[512,2048]{1,0:T(8,128)(2,1)} %a_hbm.1, f32[16,128]{1,0:T(8,128)} %targets_hbm.1, f32[2048,128]{1,0:T(8,128)} %linear_hbm.1, f32[16,128]{1,0:T(8,128)} %bitcast.1, s32[2048,128]{1,0:T(8,128)} %lower_hbm.1, s32[2048,128]{1,0:T(8,128)} %upper_hbm.1), custom_call_target="tpu_custom_call" | custom-call | tf_op jit(solution)/shard_map/admm/pallas_call | solution.py:359
  100.7 1.0 copy.10
  101.7 1.0 copy.11

commit v5 on v4

--- a/solution.py
+++ b/solution.py
@@ -58,11 +58,39 @@
 def kernel(
     devices,
     a_hbm, targets_hbm, linear_hbm, diagonal_hbm, lower_hbm, upper_hbm,
-    z_hbm, u_hbm,
-    a, a_t, linear, diagonal, code, low, high, dd, ss,
-    mz, mu, cz, cu, sz, su, base, xb, pf, pb, known_a, ra, wb, known_b, window, m, targets, ga_1, ga_2, ga_3,
-    load_sem, out_sem, send_sem, recv_sem,
+    mz, mu, low, high, *rest,
 ):
+    last, rest = rest[:ITERS], rest[ITERS:]
+    (
+        a,
+        a_t,
+        linear,
+        diagonal,
+        code,
+        dd,
+        ss,
+        cz,
+        cu,
+        sz,
+        su,
+        base,
+        xb,
+        pf,
+        pb,
+        known_a,
+        ra,
+        wb,
+        known_b,
+        window,
+        m,
+        targets,
+        ga_1,
+        ga_2,
+        ga_3,
+        load_sem,
+        send_sem,
+        recv_sem,
+    ) = rest
     chips = devices // 2
     quarters = chips // WINDOW
     rows, n = a.shape
@@ -286,6 +314,8 @@
                 return (sums[0] + folded(z * z + u * u),)
             z0, u0 = (mz[0, part, :], mu[0, part, :]) if it == 1 else (sz[part, :], su[part, :])
             value = base[part, :] - ss[part, :] * gradient
+            past = [(z0, u0) if it == 1 else (mz[0, part, :], mu[0, part, :])]
+            past += [(cz[j, part, :], cu[j, part, :]) for j in range(it - 1)]
             z = jnp.minimum(jnp.maximum(value, low[part, :]), high[part, :])
             u = value - z
             mz[it, part, :] = z
@@ -294,14 +324,7 @@
             if it < ITERS - 1:
                 cz[it - 1, part, :] = dz
                 cu[it - 1, part, :] = du
-            out = []
-            for j in range(it):
-                pz, pu = (
-                    (mz[0, part, :], mu[0, part, :])
-                    if j == 0
-                    else (cz[j - 1, part, :], cu[j - 1, part, :])
-                )
-                out.append(sums[j] + folded(pz * dz + pu * du))
+            out = [sums[j] + folded(pz * dz + pu * du) for j, (pz, pu) in enumerate(past)]
             out.append(sums[it] + folded(dz * dz + du * du))
             return tuple(out)
 
@@ -336,15 +359,15 @@
                 z = z + alpha[j] * mz[j, part, :]
                 u = u + alpha[j] * mu[j, part, :]
             z = jnp.minimum(jnp.maximum(z, low[part, :]), high[part, :])
-            if it < ITERS - 1:
-                sz[part, :] = z
-                su[part, :] = u
-                xb[part, :] = (z - u).astype(BF16)
-            else:
-                z_hbm[part, :] = z
-                u_hbm[part, :] = u
+            sz[part, :] = z
+            su[part, :] = u
+            xb[part, :] = (z - u).astype(BF16)
             return carry
 
+        if it == ITERS - 1:
+            for j in range(it + 1):
+                last[j][...] = alpha[j]
+            break
         lax.fori_loop(0, n // CHUNK, combined, 0)
 
 
@@ -356,11 +379,17 @@
     others = 2 * WINDOW - 1
     full = pltpu.VMEM((n, s), F32)
     hbm = pl.BlockSpec(memory_space=pl.ANY)
-    return pl.pallas_call(
+    mz, mu, low, high, *alpha = pl.pallas_call(
         functools.partial(kernel, devices),
-        out_shape=(pltpu.VMEM((n, s), F32),) * 2,
+        out_shape=(
+            pltpu.VMEM((ITERS, n, s), F32),
+            pltpu.VMEM((ITERS, n, s), F32),
+            pltpu.VMEM((n, s), F32),
+            pltpu.VMEM((n, s), F32),
+            *[pltpu.VMEM((1, s), F32)] * ITERS,
+        ),
         in_specs=[hbm] * 6,
-        out_specs=(pl.BlockSpec(memory_space=pltpu.VMEM),) * 2,
+        out_specs=(pl.BlockSpec(memory_space=pltpu.VMEM),) * (4 + ITERS),
         scratch_shapes=[
             pltpu.VMEM((rows, n), BF16),
             pltpu.VMEM((n, rows), BF16),
@@ -369,10 +398,6 @@
             pltpu.VMEM((2, n, s), jnp.int32),
             full,
             full,
-            full,
-            full,
-            pltpu.VMEM((ITERS, n, s), F32),
-            pltpu.VMEM((ITERS, n, s), F32),
             pltpu.VMEM((ITERS - 2, n, s), F32),
             pltpu.VMEM((ITERS - 2, n, s), F32),
             full,
@@ -392,12 +417,11 @@
             pltpu.VMEM((devices, 3, s), F32),
             pltpu.VMEM((devices, 4, s), F32),
             pltpu.SemaphoreType.DMA((6,)),
-            pltpu.SemaphoreType.DMA((2,)),
             pltpu.SemaphoreType.DMA((5,)),
             pltpu.SemaphoreType.DMA((5,)),
         ],
         compiler_params=pltpu.CompilerParams(
-            collective_id=0, has_side_effects=True, vmem_limit_bytes=56 * 1024 * 1024
+            collective_id=0, has_side_effects=True, vmem_limit_bytes=53 * 1024 * 1024
         ),
         name="admm",
     )(
@@ -408,6 +432,10 @@
         lower_code,
         upper_code,
     )
+    z, u = alpha[0] * mz[0], alpha[0] * mu[0]
+    for j in range(1, ITERS):
+        z, u = z + alpha[j] * mz[j], u + alpha[j] * mu[j]
+    return jnp.minimum(jnp.maximum(z, low), high), u
 
 
 def solution(mesh):

time: 103 us -> 102 us (level)
  local copies, waits for them, and re-layouts: 1.94 us -> 0 us
  other arithmetic: 0 us -> 1.87 us
    unnamed x2 -> x0, local copies, waits for them, and re-layouts: 1.94 us -> none
    add x0 -> x1, other arithmetic: none -> 1.87 us  [per_device(): z, u = (z + alpha[j] * mz[j], u + alpha[j] * mu[j])]
where the time goes in v5:
time: 102 us
  Pallas kernels  99.7 us (98%)
  other arithmetic  1.87 us (2%)
    pallas_call x1, Pallas kernels, per_device(): pl.pallas_call(functools.partial(kernel, devices), out_shape=(pltpu.VMEM(...  99.7 us

profile of v5, /device:TPU:69, one launch (start us, length us, event | category | flops | bytes accessed | tf_op | source)
XLA Modules:
  0.0 102.2 jit_solution(16078514921255352150)
XLA Ops:
  0.6 99.7 %admm.1 = (f32[4,2048,128]{2,1,0:T(8,128)S(1)}, f32[4,2048,128]{2,1,0:T(8,128)S(1)}, f32[2048,128]{1,0:T(8,128)S(1)}, f32[2048,128]{1,0:T(8,128)S(1)}, f32[1,128...) custom-call(bf16[512,2048]{1,0:T(8,128)(2,1)} %a_hbm.1, ...), custom_call_target="tpu_custom_call" | custom-call | tf_op jit(solution)/shard_map/admm/pallas_call | solution.py:382
  100.3 1.9 %fusion = (f32[2048,128]{1,0:T(8,128)}, f32[2048,128]{1,0:T(8,128)}) fusion(f32[4,2048,128]{2,1,0:T(8,128)S(1)} %get-tuple-element.17, f32[128]{0:T(128)S(1)} %bitcast.52, f32[128]{0:T(128)S(1)} %bitcast.51, f32[128]{0:T(128)S(1)} %bitcast.50, f32[128]{0:T(128)S(1)} %bitcast.49, f32[2048,128]{1,0:T(8,128)S(1)} %get-tuple-element.16, ...), kind=kLoop, calls=%fused_computation.1 | loop fusion | flops 4194304 | bytes 12584960 | tf_op jit(solution)/shard_map/add | solution.py:437

commit v6 on v5

--- a/solution.py
+++ b/solution.py
@@ -299,7 +299,6 @@
                 send(m.at[mine], m.at[mine], device, 3, 3)
             left(wb.at[pl.ds(0, quarters - 1)], 2)
             arrived(m.at[pl.ds(0, rows - block)], 3)
-            left(m.at[pl.ds(0, rows - block)], 3)
 
         def mapped(i, sums):
             part = pl.ds(pl.multiple_of(i * CHUNK, CHUNK), CHUNK)
@@ -330,6 +329,8 @@
 
         zero = jnp.zeros((8, s), F32)
         sums = lax.fori_loop(0, n // CHUNK, mapped, (zero,) * (it + 1))
+        if it > 0:
+            left(m.at[pl.ds(0, rows - block)], 3)
         sums = [jnp.sum(item, axis=0, keepdims=True) for item in sums]
         if it == 0:
             first = sums[0]
@@ -341,7 +342,6 @@
         everyone(ga.at[me], ga.at[me], 4)
         arrived(ga.at[pl.ds(0, devices - 1)], 4)
         total = jnp.sum(ga[...], axis=0)
-        left(ga.at[pl.ds(0, devices - 1)], 4)
         lines = [total[i : i + 1, :] for i in range(len(shared))]
         if it == 1:
             gram = [[lines[0]]]
@@ -367,8 +367,10 @@
         if it == ITERS - 1:
             for j in range(it + 1):
                 last[j][...] = alpha[j]
+            left(ga.at[pl.ds(0, devices - 1)], 4)
             break
         lax.fori_loop(0, n // CHUNK, combined, 0)
+        left(ga.at[pl.ds(0, devices - 1)], 4)
 
 
 def per_device(devices, design_matrix, targets, linear, diagonal, lower_code, upper_code):

time: 102 us -> 102 us (level)
  no operation moved by 1% of the time
where the time goes in v6:
time: 102 us
  Pallas kernels  99.9 us (98%)
  other arithmetic  1.87 us (2%)
    pallas_call x1, Pallas kernels, per_device(): pl.pallas_call(functools.partial(kernel, devices), out_shape=(pltpu.VMEM(...  99.9 us

profile of v6, /device:TPU:69, one launch (start us, length us, event | category | flops | bytes accessed | tf_op | source)
XLA Modules:
  0.0 102.4 jit_solution(13049275900824981118)
XLA Ops:
  0.6 99.9 %admm.1 = (f32[4,2048,128]{2,1,0:T(8,128)S(1)}, f32[4,2048,128]{2,1,0:T(8,128)S(1)}, f32[2048,128]{1,0:T(8,128)S(1)}, f32[2048,128]{1,0:T(8,128)S(1)}, f32[1,128...) custom-call(bf16[512,2048]{1,0:T(8,128)(2,1)} %a_hbm.1, ...), custom_call_target="tpu_custom_call" | custom-call | tf_op jit(solution)/shard_map/admm/pallas_call | solution.py:384
  100.5 1.9 %fusion = (f32[2048,128]{1,0:T(8,128)}, f32[2048,128]{1,0:T(8,128)}) fusion(f32[4,2048,128]{2,1,0:T(8,128)S(1)} %get-tuple-element.17, f32[128]{0:T(128)S(1)} %bitcast.52, f32[128]{0:T(128)S(1)} %bitcast.51, f32[128]{0:T(128)S(1)} %bitcast.50, f32[128]{0:T(128)S(1)} %bitcast.49, f32[2048,128]{1,0:T(8,128)S(1)} %get-tuple-element.16, ...), kind=kLoop, calls=%fused_computation.1 | loop fusion | flops 4194304 | bytes 12584960 | tf_op jit(solution)/shard_map/add | solution.py:439
